TPU v7x, 32 devices: a whole 2x2x4 slice. The times are simulated.
32 devices in a mesh: row: 8 (over z, x), col: 4 (over y, core).
Axes of the slice: x: 2, y: 2, z: 4, core: 2. Of those that a mesh axis runs over, the one named last changes fastest.
Arguments:
- coeffs: bfloat16 [1024, 128, 128], P(('row', 'col')), as said below
- tiles: int32 [1024, 1], replicated, may hold values from 0 to 7; in each aligned block of 32 rows (0 to 31, 32 to 63, ...) at most 5 rows name the same one
- primal: bfloat16 [1024, 1024], replicated, as said below
- dual_inverse: bfloat16 [1024, 1024], replicated, as said below
Outputs:
- schur: float32 [1024, 1024], P('row', 'col')
Inputs may be any that keep to these rules, and one draw needn't show every extreme that they name: `tiles`: within each aligned block of 32 constraints (the constraints of one device) no tile is named more than 5 times, a bound that some block reaches. Each coeffs[i] is symmetric. `primal`: Symmetric. `dual_inverse`: Symmetric.
All inputs are finite; a program needn't handle non-finite values.
Results may differ from a plain program's by a relative error of at most 0.0022.
Values may be sent and summed in bfloat16 or wider, within the bound.
A program may use at most 128 MiB of HBM per device.

v0:
```python
import jax
import jax.numpy as jnp
from jax import lax
from jax.sharding import PartitionSpec as P

MOST = 5


def slot_ranks(tile_group, first_tile, tile_width):
    labels = first_tile + jnp.arange(tile_width, dtype=jnp.int32)
    member = (tile_group[:, :, None] == labels[None, None, :]).astype(jnp.int32)
    before = jnp.cumsum(member, axis=1) - member
    return (member, jnp.sum(before * member, axis=2))


def slot_picks(tile_group, first_tile, tile_width, slot_depth):
    member, ordinal = slot_ranks(tile_group, first_tile, tile_width)
    levels = jnp.arange(slot_depth, dtype=jnp.int32)
    chosen = member[:, :, :, None] * (
        ordinal[:, :, None, None] == levels[None, None, None, :]
    ).astype(jnp.int32)
    return jnp.transpose(chosen, (0, 2, 3, 1)).astype(jnp.bfloat16)


def shards(coeffs, tiles, primal, dual_inverse):
    col_size = lax.axis_size("col")
    row_size = lax.axis_size("row")
    col_index = lax.axis_index("col")
    row_index = lax.axis_index("row")
    own_count = coeffs.shape[0]
    tile_size = coeffs.shape[1]
    tile_count = primal.shape[0] // tile_size
    per_col = tile_count // col_size
    slot_depth = MOST
    tile_area = tile_size * tile_size
    tile_ids = tiles[:, 0]
    row_count = col_size * own_count
    first_tile = col_index * per_col
    row_coeffs = lax.all_gather(coeffs, "col", axis=0, tiled=True)
    row_tiles = lax.dynamic_slice_in_dim(tile_ids, row_index * row_count, row_count)
    primal_strip = lax.dynamic_slice_in_dim(primal, first_tile * tile_size, per_col * tile_size, 1)
    primal_strip = primal_strip.reshape(tile_count, tile_size, per_col, tile_size)
    primal_pick = jnp.take(primal_strip, row_tiles, axis=0)
    product_tile = jnp.einsum(
        "iab,ibvc->ivac", row_coeffs, primal_pick, preferred_element_type=jnp.float32
    ).astype(jnp.bfloat16)
    dual_strip = lax.dynamic_slice_in_dim(
        dual_inverse, first_tile * tile_size, per_col * tile_size, 0
    )
    dual_strip = dual_strip.reshape(per_col, tile_size, tile_count, tile_size)
    dual_pick = jnp.take(dual_strip, row_tiles, axis=2)
    reduced = jnp.einsum(
        "ivba,vcib->ivac", product_tile, dual_pick, preferred_element_type=jnp.float32
    ).astype(jnp.bfloat16)
    reduced = reduced.reshape(row_count, per_col, tile_area)
    chosen_slots = slot_picks(
        row_tiles.reshape(col_size, own_count), first_tile, per_col, slot_depth
    )
    routed = jnp.einsum(
        "gvqk,gkx->gvqx",
        chosen_slots,
        row_coeffs.reshape(col_size, own_count, tile_area),
        preferred_element_type=jnp.float32,
    ).astype(jnp.bfloat16)
    values = jnp.einsum(
        "ivx,svqx->isvq",
        reduced,
        lax.all_gather(routed, "row", axis=0, tiled=True),
        preferred_element_type=jnp.float32,
    )
    home_span = row_size * per_col * slot_depth
    values = values.reshape(row_count, col_size, home_span)
    landed = lax.all_to_all(values, "col", split_axis=1, concat_axis=1, tiled=True)
    landed = landed.reshape(row_count, col_size * home_span)
    home_tiles = lax.dynamic_slice_in_dim(
        tile_ids, col_index * row_size * own_count, row_size * own_count
    )
    home_tiles = home_tiles.reshape(row_size, own_count)
    member, ordinal = slot_ranks(home_tiles, 0, tile_count)
    owner_col = home_tiles // per_col
    within = home_tiles - owner_col * per_col
    sender = jnp.arange(row_size, dtype=jnp.int32)[:, None]
    column_pick = (
        owner_col * home_span + sender * (per_col * slot_depth) + within * slot_depth + ordinal
    )
    return jnp.take(landed, column_pick.reshape(-1), axis=1)


def solution(mesh):
    return jax.shard_map(
        shards,
        mesh=mesh,
        in_specs=(P(("row", "col"), None, None), P(), P(), P()),
        out_specs=P("row", "col"),
        check_vma=False,
    )
```

profile of v0, /device:TPU:0, one launch (start us, length us, event | category | flops | bytes accessed | tf_op | source)
XLA Modules:
  0.0 243.5 jit_solution(329211813767962392)
XLA Ops:
  6.5 0.7 all-gather.3.cloned.1.call-update
  7.3 0.7 fusion.41
  8.2 0.2 fusion.35
  8.5 37.6 %all-gather.3.cloned.1.call-done = bf16[128,128,128]{2,1,0:T(8,128)(2,1)} async-done(((bf16[32,128,128]{2,1,0:T(8,128)(2,1)}), bf16[128,128,128]{2,1,0:T(8,128)(2,1)}) %all-gather.3.cloned.1.call-update) | async-done | bytes 4194320 | tf_op jit(solution)/shard_map/all_gather | solution.py:39
  46.1 7.3 %reshape.93 = bf16[4,32,16384,1]{2,1,0,3:T(8,128)(2,1)} reshape(bf16[128,128,128]{2,1,0:T(8,128)(2,1)} %all-gather.3.cloned.1.call-done) | data formatting | bytes 8388608 | tf_op jit(solution)/shard_map/reshape | solution.py:62
  53.4 2.9 %convolution_convert_fusion = bf16[4,2,5,16384]{3,2,1,0:T(8,128)(2,1)S(1)} fusion(bf16[4,32,16384,1]{2,1,0,3:T(8,128)(2,1)} %reshape.93, s32[4,5,32]{2,1,0:T(8,128)S(1)} %fusion.39, s32[4,2,32]{2,1,0:T(2,128)S(1)} %compare_convert_fusion.1), kind=kOutput, calls=%fused_computation.3 | convolution fusion | flops 42600960 | bytes 5508608 | tf_op jit(solution)/shard_map/gvqk,gkx->gvqx/dot_general | solution.py:59
  56.3 2.6 %copy.45 = bf16[4,2,5,16384]{3,1,2,0:T(2,128)(2,1)} copy(bf16[4,2,5,16384]{3,2,1,0:T(8,128)(2,1)S(1)} %convolution_convert_fusion) | data formatting | bytes 2621440 | tf_op jit(solution)/shard_map/convert_element_type | solution.py:64
  59.0 0.1 reshape.97
  59.2 0.1 copy.47
  59.3 1.1 dynamic-slice_bitcast_fusion
  60.6 6.7 %gather_fusion = bf16[128,128,2,128]{3,1,2,0:T(8,128)(2,1)} fusion(bf16[8,128,2,128]{3,1,2,0:T(8,128)(2,1)S(1)} %copy.47, s32[1024]{0:T(1024)S(1)} %pad_clamp_fusion.1), kind=kCustom, calls=%fused_computation | custom fusion | bytes 16777728 | tf_op jit(solution)/shard_map/jit(_take)/gather | solution.py:43
  67.3 6.7 %gather_fusion.1 = bf16[128,2,128,128]{3,2,1,0:T(8,128)(2,1)} fusion(bf16[2,128,8,128]{3,1,2,0:T(8,128)(2,1)S(1)} %copy.49, s32[1024]{0:T(1024)S(1)} %pad_clamp_fusion.1), kind=kCustom, calls=%fused_computation.1 | custom fusion | bytes 16777728 | tf_op jit(solution)/shard_map/jit(_take)/gather | solution.py:51
  74.1 0.7 fusion.44
  75.2 15.0 %fusion.11 = bf16[128,2,128,128]{3,2,1,0:T(8,128)(2,1)} fusion(bf16[128,2,128,128]{3,2,1,0:T(8,128)(2,1)} %gather_fusion.1, pred[128]{0:T(512)(128)(4,1)S(1)} %get-tuple-element.7, bf16[128,128,2,128]{3,1,2,0:T(8,128)(2,1)} %gather_fusion, bf16[128,128,128]{2,1,0:T(8,128)(2,1)} %all-gather.3.cloned.1.call-done), kind=kOutput, calls=%fused_computation.15 | convolution fusion | flops 2164260864 | bytes 29360256 | tf_op jit(solution)/shard_map/ivba,vcib->ivac/dot_general | solution.py:52
  90.2 12.6 %reshape.66 = bf16[128,2,16384]{2,1,0:T(2,128)(2,1)} reshape(bf16[128,2,128,128]{3,2,1,0:T(8,128)(2,1)} %fusion.11) | data formatting | bytes 16777216 | tf_op jit(solution)/shard_map/reshape | solution.py:55
  102.7 106.9 %all-gather.5.cloned.1.call-done = bf16[32,2,5,16384]{3,1,2,0:T(2,128)(2,1)} async-done(((bf16[4,2,5,16384]{3,1,2,0:T(2,128)(2,1)}), bf16[32,2,5,16384]{3,1,2,0:T(2,128)(2,1)}) %all-gather.5.cloned.1.call-update) | async-done | bytes 10485776 | tf_op jit(solution)/shard_map/all_gather | solution.py:68
  209.6 16.4 %fusion.28 = f32[128,32,2,5]{0,1,3,2:T(8,128)S(1)} fusion(bf16[128,2,16384,1]{2,1,0,3:T(2,128)(2,1)} %bitcast.36, bf16[32,2,5,16384]{3,1,2,0:T(2,128)(2,1)} %all-gather.5.cloned.1.call-done), kind=kOutput, calls=%fused_computation.20 | convolution fusion | flops 1342177280 | bytes 19038208 | tf_op jit(solution)/shard_map/ivx,svqx->isvq/dot_general | solution.py:65
  226.0 0.1 copy.52
  226.1 0.7 reshape.67
  226.8 3.3 %all-to-all-start = ((f32[128,4,80]{0,2,1:T(8,128)}), f32[128,4,80]{0,2,1:T(8,128)S(1)}, u32[]{:S(2)}, u32[]{:S(2)}) async-start(f32[128,4,80]{0,2,1:T(8,128)} %reshape.67), calls=%async_computation | async-start | bytes 327680 | tf_op jit(solution)/shard_map/all_to_all | solution.py:73
  230.2 4.9 %all-to-all-done = f32[128,4,80]{0,2,1:T(8,128)S(1)} async-done(((f32[128,4,80]{0,2,1:T(8,128)}), f32[128,4,80]{0,2,1:T(8,128)S(1)}, u32[]{:S(2)}, u32[]{:S(2)}) %all-to-all-start) | async-done | bytes 163872 | tf_op jit(solution)/shard_map/all_to_all | solution.py:73
  235.0 0.7 gather_fusion.2
  235.8 0.1 select_bitcast_fusion
  235.9 0.8 copy.53
  (28 shorter events, 1.2 us)
Async XLA Ops:
  6.5 52.4 %copy-start = (bf16[1024,1024]{1,0:T(8,128)(2,1)S(1)}, bf16[1024,1024]{1,0:T(8,128)(2,1)}, u32[]{:S(2)}) copy-start(bf16[1024,1024]{1,0:T(8,128)(2,1)} %param.6) | copy-start | bytes 6291460
  6.5 39.6 %all-gather.3.cloned.1.call-start = ((), (), s32[]{:S(2)}) async-start(), calls=%async_computation.1 | async-start | bytes 5242880 | tf_op jit(solution)/shard_map/all_gather | solution.py:39
  7.3 202.3 %all-gather.5.cloned.1.call-start = ((), (), s32[]{:S(2)}) async-start(), calls=%async_computation.2 | async-start | bytes 11796480 | tf_op jit(solution)/shard_map/all_gather | solution.py:68
  53.4 7.1 %copy-start.1 = (s32[1024,1]{0,1:T(1,128)S(1)}, s32[1024,1]{0,1:T(1,128)}, u32[]{:S(2)}) copy-start(s32[1024,1]{0,1:T(1,128)} %param.5) | copy-start | bytes 12292
  226.8 8.3 %all-to-all-start = ((f32[128,4,80]{0,2,1:T(8,128)}), f32[128,4,80]{0,2,1:T(8,128)S(1)}, u32[]{:S(2)}, u32[]{:S(2)}) async-start(f32[128,4,80]{0,2,1:T(8,128)} %reshape.67), calls=%async_computation | async-start | bytes 327680 | tf_op jit(solution)/shard_map/all_to_all | solution.py:73
Sparse Core Ops, SparseCore 0:
  8.9 37.1 all-gather.2
  59.0 150.4 all-gather.4
where the time goes:
time: 244 us; the launch traced here: 243 us
  waiting for transfers between devices  150 us (61%)
  local copies, waits for them, and re-layouts  40.9 us (17%)
  matrix products  34.2 us (14%)
  between operations  13.5 us (6%)
  starting transfers between devices  3.39 us (1%)
    all_gather x1, waiting for transfers between devices, shards(): lax.all_gather(routed, 'row', axis=0, tiled=True)  107 us
    all_gather x1, waiting for transfers between devices, shards(): row_coeffs = lax.all_gather(coeffs, 'col', axis=0, tiled=True)  37.6 us
    dot_general x1, matrix products, shards(): jnp.einsum('ivx,svqx->isvq', reduced, lax.all_gather(routed, 'row', axis=...  16.4 us
    dot_general x1, matrix products, shards(): jnp.einsum('ivba,vcib->ivac', product_tile, dual_pick, preferred_element_...  15 us
    reshape x1, local copies, waits for them, and re-layouts, shards(): reduced = reduced.reshape(row_count, per_col, tile_area)  12.6 us
    reshape x1, local copies, waits for them, and re-layouts, shards(): row_coeffs.reshape(col_size, own_count, tile_area)  7.31 us
    gather x1, local copies, waits for them, and re-layouts, shards(): primal_pick = jnp.take(primal_strip, row_tiles, axis=0)  6.69 us
    gather x1, local copies, waits for them, and re-layouts, shards(): dual_pick = jnp.take(dual_strip, row_tiles, axis=2)  6.68 us
  transfers between devices with their start and end apart: 3, of which 3 were waited for; matrix products, arithmetic and copies ran while one was open for 18% of the time, Pallas kernels for 0%

commit v1 on v0

--- a/solution.py
+++ b/solution.py
@@ -4,6 +4,19 @@
 from jax.sharding import PartitionSpec as P
 
 MOST = 5
+
+
+def gather_around(value, axis, dim):
+    ways = lax.axis_size(axis)
+    up = [(d, (d + 1) % ways) for d in range(ways)]
+    down = [(d, (d - 1) % ways) for d in range(ways)]
+    earlier, later = ([value], [value])
+    for _ in range(ways // 2):
+        earlier.append(lax.ppermute(earlier[-1], axis, up))
+    for _ in range((ways - 1) // 2):
+        later.append(lax.ppermute(later[-1], axis, down))
+    line = jnp.concatenate([*earlier[::-1], *later[1:]], axis=dim)
+    return jnp.roll(line, (lax.axis_index(axis) - ways // 2) * value.shape[dim], axis=dim)
 
 
 def slot_ranks(tile_group, first_tile, tile_width):
@@ -65,7 +78,7 @@
     values = jnp.einsum(
         "ivx,svqx->isvq",
         reduced,
-        lax.all_gather(routed, "row", axis=0, tiled=True),
+        gather_around(routed, "row", 0),
         preferred_element_type=jnp.float32,
     )
     home_span = row_size * per_col * slot_depth

time: 244 us -> 332 us (1.36)
  local copies, waits for them, and re-layouts: 40.9 us -> 74.8 us
  starting transfers between devices: 3.39 us -> 29 us
  waiting for transfers between devices: 150 us -> 169 us
  matrix products: 34.2 us -> 42.7 us
    ppermute x0 -> x7, waiting for transfers between devices: none -> 126 us  [the longest x4 110 us: gather_around(): earlier.append(lax.ppermute(earlier[-1], axis, up))]
    all_gather x1 -> x0, waiting for transfers between devices: 107 us -> none  [shards(): lax.all_gather(routed, 'row', axis=0, tiled=True)]
    ppermute x0 -> x7, starting transfers between devices: none -> 25.6 us  [the longest x3 19.1 us: gather_around(): later.append(lax.ppermute(later[-1], axis, down))]
    unnamed x6 -> x31, local copies, waits for them, and re-layouts: 1.18 us -> 25.8 us
    dot_general x1, matrix products: 16.4 us -> 24.9 us  [shards(): jnp.einsum('ivx,svqx->isvq', reduced, gather_around(routed, 'row', 0), pr...]
    dynamic_slice x0 -> x1, local copies, waits for them, and re-layouts: none -> 7.41 us  [gather_around(): jnp.roll(line, (lax.axis_index(axis) - ways // 2) * value.shape[dim], axi...]
  transfers between devices with their start and end apart: 3 -> 9, of which waited for: 3 -> 6; matrix products, arithmetic and copies ran while one was open for 18% -> 17% of each run, Pallas kernels for 0% -> 0%
where the time goes in v1:
time: 332 us; the launch traced here: 331 us
  waiting for transfers between devices  169 us (51%)
  local copies, waits for them, and re-layouts  74.8 us (23%)
  matrix products  42.7 us (13%)
  starting transfers between devices  29 us (9%)
  between operations  13.6 us (4%)
    ppermute x4, waiting for transfers between devices, gather_around(): earlier.append(lax.ppermute(earlier[-1], axis, up))  110 us
    all_gather x1, waiting for transfers between devices, shards(): row_coeffs = lax.all_gather(coeffs, 'col', axis=0, tiled=True)  37.6 us
    unnamed x31, local copies, waits for them, and re-layouts  25.8 us
    dot_general x1, matrix products, shards(): jnp.einsum('ivx,svqx->isvq', reduced, gather_around(routed, 'row', 0), pr...  24.9 us
    ppermute x3, starting transfers between devices, gather_around(): later.append(lax.ppermute(later[-1], axis, down))  19.1 us
    ppermute x3, waiting for transfers between devices, gather_around(): later.append(lax.ppermute(later[-1], axis, down))  16.4 us
    dot_general x1, matrix products, shards(): jnp.einsum('ivba,vcib->ivac', product_tile, dual_pick, preferred_element_...  14.9 us
    reshape x1, local copies, waits for them, and re-layouts, shards(): reduced = reduced.reshape(row_count, per_col, tile_area)  12.5 us
  transfers between devices with their start and end apart: 9, of which 6 were waited for; matrix products, arithmetic and copies ran while one was open for 17% of the time, Pallas kernels for 0%

profile of v1, /device:TPU:0, one launch (start us, length us, event | category | flops | bytes accessed | tf_op | source)
XLA Modules:
  0.0 330.8 jit_solution(8297377580957259672)
XLA Ops:
  8.5 37.6 %all-gather.2.cloned.1.call-done = bf16[128,128,128]{2,1,0:T(8,128)(2,1)} async-done(((bf16[32,128,128]{2,1,0:T(8,128)(2,1)}), bf16[128,128,128]{2,1,0:T(8,128)(2,1)}) %all-gather.2.cloned.1.call-update) | async-done | bytes 4194320 | tf_op jit(solution)/shard_map/all_gather | solution.py:52
  46.1 7.3 %reshape.93 = bf16[4,32,16384,1]{2,1,0,3:T(8,128)(2,1)} reshape(bf16[128,128,128]{2,1,0:T(8,128)(2,1)} %all-gather.2.cloned.1.call-done) | data formatting | bytes 8388608 | tf_op jit(solution)/shard_map/reshape | solution.py:75
  53.4 2.9 convolution_convert_fusion
  57.6 2.2 copy.62
  61.3 32.4 %collective-permute-done = bf16[4,2,5,16384]{3,0,2,1:T(4,128)(2,1)S(1)} collective-permute-done((bf16[4,2,5,16384]{3,0,2,1:T(4,128)(2,1)}, bf16[4,2,5,16384]{3,0,2,1:T(4,128)(2,1)S(1)}, u32[]{:S(2)}, u32[]{:S(2)}) %collective-permute-start) | collective-permute-done | bytes 1310752 | tf_op jit(solution)/shard_map/ppermute | solution.py:15
  93.7 4.7 %collective-permute-start.4 = (bf16[4,2,5,16384]{3,0,2,1:T(4,128)(2,1)}, bf16[4,2,5,16384]{3,0,2,1:T(4,128)(2,1)}, u32[]{:S(2)}, u32[]{:S(2)}) collective-permute-start(bf16[4,2,5,16384]{3,0,2,1:T(4,128)(2,1)} %copy.62), channel_id=1, source_target_pairs={{0,28},{4,0},{8,4},{12,8},{16,12},{20,16},{24,20},{28,24},{1,29},{... | collective-permute-start | bytes 3932168 | tf_op jit(solution)/shard_map/ppermute | solution.py:17
  98.4 51.2 %collective-permute-done.1 = bf16[4,2,5,16384]{3,0,2,1:T(4,128)(2,1)} collective-permute-done((bf16[4,2,5,16384]{3,0,2,1:T(4,128)(2,1)S(1)}, bf16[4,2,5,16384]{3,0,2,1:T(4,128)(2,1)}, u32[]{:S(2)}, u32[]{:S(2)}) %collective-permute-start.1) | collective-permute-done | bytes 1310752 | tf_op jit(solution)/shard_map/ppermute | solution.py:15
  149.6 2.6 collective-permute-start.2
  155.7 6.6 %gather_fusion = bf16[128,128,2,128]{3,1,2,0:T(8,128)(2,1)} fusion(bf16[8,128,2,128]{3,1,2,0:T(8,128)(2,1)S(1)} %copy.79, s32[1024]{0:T(1024)S(1)} %pad_clamp_fusion.1), kind=kCustom, calls=%fused_computation | custom fusion | bytes 16777728 | tf_op jit(solution)/shard_map/jit(_take)/gather | solution.py:56
  162.3 6.6 %gather_fusion.1 = bf16[128,2,128,128]{3,2,1,0:T(8,128)(2,1)} fusion(bf16[2,128,8,128]{3,1,2,0:T(8,128)(2,1)S(1)} %copy.81, s32[1024]{0:T(1024)S(1)} %pad_clamp_fusion.1), kind=kCustom, calls=%fused_computation.1 | custom fusion | bytes 16777728 | tf_op jit(solution)/shard_map/jit(_take)/gather | solution.py:64
  170.1 11.4 %collective-permute-start.5 = (bf16[4,2,5,16384]{3,0,2,1:T(4,128)(2,1)}, bf16[4,2,5,16384]{3,0,2,1:T(4,128)(2,1)}, u32[]{:S(2)}, u32[]{:S(2)}) collective-permute-start(bf16[4,2,5,16384]{3,0,2,1:T(4,128)(2,1)} %collective-permute-done.4), channel_id=1, source_target_pairs={{0,28},{4,0},{8,4},{12,8},{16,12},{20,16},{24,20},{28,24},{1,29},{... | collective-permute-start | bytes 3932168 | tf_op jit(solution)/shard_map/ppermute | solution.py:17
  181.5 26.2 %collective-permute-done.2 = bf16[4,2,5,16384]{3,0,2,1:T(4,128)(2,1)} collective-permute-done((bf16[4,2,5,16384]{3,0,2,1:T(4,128)(2,1)}, bf16[4,2,5,16384]{3,0,2,1:T(4,128)(2,1)}, u32[]{:S(2)}, u32[]{:S(2)}) %collective-permute-start.2) | collective-permute-done | bytes 1310752 | tf_op jit(solution)/shard_map/ppermute | solution.py:15
  207.6 2.5 collective-permute-start.3
  210.1 14.9 %fusion.11 = bf16[128,2,128,128]{3,2,1,0:T(8,128)(2,1)} fusion(bf16[128,2,128,128]{3,2,1,0:T(8,128)(2,1)} %gather_fusion.1, pred[128]{0:T(512)(128)(4,1)S(1)} %get-tuple-element.7, bf16[128,128,2,128]{3,1,2,0:T(8,128)(2,1)} %gather_fusion, bf16[128,128,128]{2,1,0:T(8,128)(2,1)} %all-gather.2.cloned.1.call-done), kind=kOutput, calls=%fused_computation.15 | convolution fusion | flops 2164260864 | bytes 29360256 | tf_op jit(solution)/shard_map/ivba,vcib->ivac/dot_general | solution.py:65
  225.0 12.5 %reshape.66 = bf16[128,2,16384]{2,1,0:T(2,128)(2,1)} reshape(bf16[128,2,128,128]{3,2,1,0:T(8,128)(2,1)} %fusion.11) | data formatting | bytes 16777216 | tf_op jit(solution)/shard_map/reshape | solution.py:68
  237.5 3.0 collective-permute-start.6
  240.5 2.1 copy_dynamic-update-slice_fusion.12
  242.6 2.1 copy_dynamic-update-slice_fusion.10
  247.7 2.1 copy_dynamic-update-slice_fusion.4
  251.8 16.4 %collective-permute-done.6 = bf16[4,2,5,16384]{3,0,2,1:T(4,128)(2,1)S(1)} collective-permute-done((bf16[4,2,5,16384]{3,0,2,1:T(4,128)(2,1)}, bf16[4,2,5,16384]{3,0,2,1:T(4,128)(2,1)S(1)}, u32[]{:S(2)}, u32[]{:S(2)}) %collective-permute-start.6) | collective-permute-done | bytes 1310752 | tf_op jit(solution)/shard_map/ppermute | solution.py:17
  281.0 7.4 %constant_dynamic-slice_fusion.1 = bf16[32,2,5,16384]{3,2,1,0:T(8,128)(2,1)} fusion(bf16[64,2,5,16384]{3,2,1,0:T(8,128)(2,1)S(1)} %copy_dynamic-update-slice_fusion.1, s32[]{:T(128)S(6)} %select_n.62), kind=kLoop, calls=%fused_computation.64 | loop fusion | bytes 20971524 | tf_op jit(solution)/shard_map/jit(_roll_dynamic)/dynamic_slice | solution.py:19
  288.4 24.9 %fusion.28 = f32[128,32,2,5]{0,1,3,2:T(8,128)S(1)} fusion(bf16[128,2,16384,1]{2,1,0,3:T(2,128)(2,1)S(1)} %bitcast.38, bf16[32,2,5,16384]{3,2,1,0:T(8,128)(2,1)} %constant_dynamic-slice_fusion.1), kind=kOutput, calls=%fused_computation.34 | convolution fusion | flops 1342177280 | bytes 19038208 | tf_op jit(solution)/shard_map/ivx,svqx->isvq/dot_general | solution.py:78
  314.1 3.3 %all-to-all-start = ((f32[128,4,80]{0,2,1:T(8,128)}), f32[128,4,80]{0,2,1:T(8,128)S(1)}, u32[]{:S(2)}, u32[]{:S(2)}) async-start(f32[128,4,80]{0,2,1:T(8,128)} %reshape.67), calls=%async_computation | async-start | bytes 327680 | tf_op jit(solution)/shard_map/all_to_all | solution.py:86
  317.5 4.9 %all-to-all-done = f32[128,4,80]{0,2,1:T(8,128)S(1)} async-done(((f32[128,4,80]{0,2,1:T(8,128)}), f32[128,4,80]{0,2,1:T(8,128)S(1)}, u32[]{:S(2)}, u32[]{:S(2)}) %all-to-all-start) | async-done | bytes 163872 | tf_op jit(solution)/shard_map/all_to_all | solution.py:86
  (67 shorter events, 29.6 us)
Async XLA Ops:
  6.5 145.7 %copy-start = (bf16[1024,1024]{1,0:T(8,128)(2,1)S(1)}, bf16[1024,1024]{1,0:T(8,128)(2,1)}, u32[]{:S(2)}) copy-start(bf16[1024,1024]{1,0:T(8,128)(2,1)} %param.6) | copy-start | bytes 6291460
  6.5 39.6 %all-gather.2.cloned.1.call-start = ((), (), s32[]{:S(2)}) async-start(), calls=%async_computation.1 | async-start | bytes 5242880 | tf_op jit(solution)/shard_map/all_gather | solution.py:52
  53.4 102.2 %copy-start.4 = (s32[1024,1]{0,1:T(1,128)S(1)}, s32[1024,1]{0,1:T(1,128)}, u32[]{:S(2)}) copy-start(s32[1024,1]{0,1:T(1,128)} %param.5) | copy-start | bytes 12292
  56.3 1.3 copy-start.2
  59.8 33.8 %collective-permute-start = (bf16[4,2,5,16384]{3,0,2,1:T(4,128)(2,1)}, bf16[4,2,5,16384]{3,0,2,1:T(4,128)(2,1)S(1)}, u32[]{:S(2)}, u32[]{:S(2)}) collective-permute-start(bf16[4,2,5,16384]{3,0,2,1:T(4,128)(2,1)} %copy.62), channel_id=1, source_target_pairs={{0,4},{4,8},{8,12},{12,16},{16,20},{20,24},{24,28},{28,0},{1,5},{5... | collective-permute-start | bytes 3932168 | tf_op jit(solution)/shard_map/ppermute | solution.py:15
  93.7 56.0 %collective-permute-start.1 = (bf16[4,2,5,16384]{3,0,2,1:T(4,128)(2,1)S(1)}, bf16[4,2,5,16384]{3,0,2,1:T(4,128)(2,1)}, u32[]{:S(2)}, u32[]{:S(2)}) collective-permute-start(bf16[4,2,5,16384]{3,0,2,1:T(4,128)(2,1)S(1)} %collective-permute-done), channel_id=1, source_target_pairs={{0,4},{4,8},{8,12},{12,16},{16,20},{20,24},{24,28},{28,0},{1,5},{5... | collective-permute-start | bytes 3932168 | tf_op jit(solution)/shard_map/ppermute | solution.py:15
  93.7 76.4 %collective-permute-start.4 = (bf16[4,2,5,16384]{3,0,2,1:T(4,128)(2,1)}, bf16[4,2,5,16384]{3,0,2,1:T(4,128)(2,1)}, u32[]{:S(2)}, u32[]{:S(2)}) collective-permute-start(bf16[4,2,5,16384]{3,0,2,1:T(4,128)(2,1)} %copy.62), channel_id=1, source_target_pairs={{0,28},{4,0},{8,4},{12,8},{16,12},{20,16},{24,20},{28,24},{1,29},{... | collective-permute-start | bytes 3932168 | tf_op jit(solution)/shard_map/ppermute | solution.py:17
  149.6 58.0 %collective-permute-start.2 = (bf16[4,2,5,16384]{3,0,2,1:T(4,128)(2,1)}, bf16[4,2,5,16384]{3,0,2,1:T(4,128)(2,1)}, u32[]{:S(2)}, u32[]{:S(2)}) collective-permute-start(bf16[4,2,5,16384]{3,0,2,1:T(4,128)(2,1)} %collective-permute-done.1), channel_id=1, source_target_pairs={{0,4},{4,8},{8,12},{12,16},{16,20},{20,24},{24,28},{28,0},{1,5},{5... | collective-permute-start | bytes 3932168 | tf_op jit(solution)/shard_map/ppermute | solution.py:15
  170.1 67.4 %collective-permute-start.5 = (bf16[4,2,5,16384]{3,0,2,1:T(4,128)(2,1)}, bf16[4,2,5,16384]{3,0,2,1:T(4,128)(2,1)}, u32[]{:S(2)}, u32[]{:S(2)}) collective-permute-start(bf16[4,2,5,16384]{3,0,2,1:T(4,128)(2,1)} %collective-permute-done.4), channel_id=1, source_target_pairs={{0,28},{4,0},{8,4},{12,8},{16,12},{20,16},{24,20},{28,24},{1,29},{... | collective-permute-start | bytes 3932168 | tf_op jit(solution)/shard_map/ppermute | solution.py:17
  207.6 32.9 %collective-permute-start.3 = (bf16[4,2,5,16384]{3,0,2,1:T(4,128)(2,1)}, bf16[4,2,5,16384]{3,0,2,1:T(4,128)(2,1)}, u32[]{:S(2)}, u32[]{:S(2)}) collective-permute-start(bf16[4,2,5,16384]{3,0,2,1:T(4,128)(2,1)} %collective-permute-done.2), channel_id=1, source_target_pairs={{0,4},{4,8},{8,12},{12,16},{16,20},{20,24},{24,28},{28,0},{1,5},{5... | collective-permute-start | bytes 3932168 | tf_op jit(solution)/shard_map/ppermute | solution.py:15
  237.5 10.0 %copy-start.3 = (bf16[4,2,5,16384]{3,2,1,0:T(8,128)(2,1)S(1)}, bf16[4,2,5,16384]{3,2,1,0:T(8,128)(2,1)}, u32[]{:S(2)}) copy-start(bf16[4,2,5,16384]{3,2,1,0:T(8,128)(2,1)} %copy-done.2) | copy-start | bytes 3932164
  237.5 30.7 %collective-permute-start.6 = (bf16[4,2,5,16384]{3,0,2,1:T(4,128)(2,1)}, bf16[4,2,5,16384]{3,0,2,1:T(4,128)(2,1)S(1)}, u32[]{:S(2)}, u32[]{:S(2)}) collective-permute-start(bf16[4,2,5,16384]{3,0,2,1:T(4,128)(2,1)} %collective-permute-done.5), channel_id=1, source_target_pairs={{0,28},{4,0},{8,4},{12,8},{16,12},{20,16},{24,20},{28,24},{1,29},{... | collective-permute-start | bytes 3932168 | tf_op jit(solution)/shard_map/ppermute | solution.py:17
  280.2 8.2 %slice-start = ((s8[8388608]{0:T(1024)(128)(4,1)}), s8[4194304]{0:T(1024)(128)(4,1)S(1)}, s32[]{:S(2)}) async-start(s8[8388608]{0:T(1024)(128)(4,1)} %bitcast.36), calls=%async_computation.2 | async-start | bytes 8388608
  281.0 7.4 %slice-start.1 = ((s8[8388608]{0:T(1024)(128)(4,1)}), s8[4194304]{0:T(1024)(128)(4,1)S(1)}, s32[]{:S(2)}) async-start(s8[8388608]{0:T(1024)(128)(4,1)} %bitcast.36), calls=%async_computation.3 | async-start | bytes 8388608
  288.4 35.6 %copy-start.1 = (bf16[1024,1024]{1,0:T(8,128)(2,1)S(1)}, bf16[1024,1024]{1,0:T(8,128)(2,1)}, u32[]{:S(2)}) copy-start(bf16[1024,1024]{1,0:T(8,128)(2,1)} %param.6) | copy-start | bytes 6291460
  314.1 8.3 %all-to-all-start = ((f32[128,4,80]{0,2,1:T(8,128)}), f32[128,4,80]{0,2,1:T(8,128)S(1)}, u32[]{:S(2)}, u32[]{:S(2)}) async-start(f32[128,4,80]{0,2,1:T(8,128)} %reshape.67), calls=%async_computation | async-start | bytes 327680 | tf_op jit(solution)/shard_map/all_to_all | solution.py:86
Sparse Core Ops, SparseCore 0:
  8.9 37.1 all-gather.1
